TPU v7x, 32 devices: a whole 2x2x4 slice. The times are simulated.
32 devices in a mesh: group: 2 (over y), ha: 4 (over x, core), wa: 4 (over z).
Axes of the slice: x: 2, y: 2, z: 4, core: 2. Of those that a mesh axis runs over, the one named last changes fastest.
Arguments:
- queries: bfloat16 [4, 32, 32, 1536], P('group', 'ha', 'wa'), parts along dimension 0, may hold values from -6 to 6
- keys: bfloat16 [4, 32, 32, 1536], P('group', 'ha', 'wa'), parts along dimension 0, may hold values from -6 to 6
- values: bfloat16 [4, 32, 32, 1536], P('group', 'ha', 'wa'), parts along dimension 0, may hold values from -6 to 6
- out_grad: bfloat16 [4, 32, 32, 1536], P('group', 'ha', 'wa'), parts along dimension 0, may hold values from -96 to 96
- log_norm: float32 [12, 4, 32, 32], P(None, 'group', 'ha', 'wa'), parts along dimension 1, may hold values from 6.5 to 7.5
- delta_rows: float32 [12, 4, 32, 32], P(None, 'group', 'ha', 'wa'), parts along dimension 1, may hold values from -360 to 360
- text_keys: bfloat16 [64, 1536], P('group'), parts along dimension 0, may hold values from -6 to 6
- text_values: bfloat16 [64, 1536], P('group'), parts along dimension 0, may hold values from -6 to 6
- window_table: int32 [4, 4, 9], replicated, may hold values 0 or 1
Outputs:
- query_grad: bfloat16 [4, 32, 32, 1536], P('group', 'ha', 'wa'), parts along dimension 0
- key_grad: bfloat16 [4, 32, 32, 1536], P('group', 'ha', 'wa'), parts along dimension 0
- value_grad: bfloat16 [4, 32, 32, 1536], P('group', 'ha', 'wa'), parts along dimension 0
- text_key_grad: bfloat16 [64, 1536], P('group'), parts along dimension 0
- text_value_grad: bfloat16 [64, 1536], P('group'), parts along dimension 0
There are 2 independent parts, one for each index of `group`. A program takes and returns all parts, laid end to end along the dimension named above; an argument that names none is the same for every part. Nothing has to cross between parts.
All inputs are finite; a program needn't handle non-finite values.
Results may differ from a plain program's by a relative error of at most 0.001.
The roundings to bfloat16 on the way count: a program that leaves them out, or rounds other values in their place, can miss the bound.
Values may be sent and summed in bfloat16 or wider, within the bound.
A program may use at most 64 MiB of HBM per device.

v0:
```python
import math
import jax
import jax.numpy as jnp
from jax import lax
from jax.sharding import PartitionSpec as P

HEADS = 12
HDIM = 128
TILE = 8
HALO = 2


def passed_along(value, axis, steps):
    count = lax.axis_size(axis)
    pairs = [(source, (source + steps) % count) for source in range(count)]
    return lax.ppermute(value, axis, pairs)


def with_halo(cells, sides, width):
    for axis, dim in sides:
        count = lax.axis_size(axis)
        head = lax.slice_in_dim(cells, 0, width, axis=dim)
        tail = lax.slice_in_dim(cells, cells.shape[dim] - width, cells.shape[dim], axis=dim)
        cells = jnp.concatenate(
            [
                lax.ppermute(tail, axis, [(i, (i + 1) % count) for i in range(count)]),
                cells,
                lax.ppermute(head, axis, [((i + 1) % count, i) for i in range(count)]),
            ],
            axis=dim,
        )
    return cells


def tile_grads(query_rows, cotangent_rows, norm_rows, delta_part, key_rows, value_rows, cell_mask):
    score_scale = 1.0 / math.sqrt(query_rows.shape[-1])
    scores = (
        jnp.einsum("qhd,khd->hqk", query_rows, key_rows, preferred_element_type=jnp.float32)
        * score_scale
    )
    probs = jnp.exp(scores - norm_rows[:, :, None])
    if cell_mask is not None:
        probs = probs * cell_mask[None, None, :]
    probs_half = probs.astype(jnp.bfloat16)
    value_part = jnp.einsum(
        "hqk,qhd->khd", probs_half, cotangent_rows, preferred_element_type=jnp.float32
    )
    prob_grad = jnp.einsum(
        "qhd,khd->hqk", cotangent_rows, value_rows, preferred_element_type=jnp.float32
    )
    score_grad = (probs * (prob_grad - delta_part[:, :, None])).astype(jnp.bfloat16)
    query_part = (
        jnp.einsum("hqk,khd->qhd", score_grad, key_rows, preferred_element_type=jnp.float32)
        * score_scale
    )
    key_part = (
        jnp.einsum("hqk,qhd->khd", score_grad, query_rows, preferred_element_type=jnp.float32)
        * score_scale
    )
    return (query_part, key_part, value_part)


def send_cols(strip, offset):
    return passed_along(strip, "wa", offset)


def send_rows(strip, offset):
    return passed_along(strip, "ha", offset)


def fold_band(buffer, along, mover):
    lower = lax.slice_in_dim(buffer, 0, HALO, axis=along)
    middle = lax.slice_in_dim(buffer, HALO, HALO + TILE, axis=along)
    upper = lax.slice_in_dim(buffer, HALO + TILE, TILE + 2 * HALO, axis=along)
    from_before = mover(upper, 1)
    from_after = mover(lower, -1)
    widths_low = [(0, 0)] * buffer.ndim
    widths_high = [(0, 0)] * buffer.ndim
    widths_low[along] = (0, TILE - HALO)
    widths_high[along] = (TILE - HALO, 0)
    return middle + jnp.pad(from_before, widths_low) + jnp.pad(from_after, widths_high)


def local(
    queries, keys, values, out_grad, log_norm, delta_rows, text_keys, text_values, window_table
):
    frames, tile_side, _, width = queries.shape
    window_side = TILE + 2 * HALO
    stacked = jnp.stack((keys, values))
    window = with_halo(stacked, (("ha", 2), ("wa", 3)), HALO)
    row_tile = lax.axis_index("ha")
    col_tile = lax.axis_index("wa")
    anchor = jnp.zeros((), jnp.int32)
    pattern = (
        lax.dynamic_slice(window_table, (row_tile, col_tile, anchor), (1, 1, 9))
        .reshape(3, 3)
        .astype(jnp.float32)
    )
    position = jnp.arange(window_side, dtype=jnp.int32)
    block_of = (position >= HALO).astype(jnp.int32) + (position >= HALO + TILE).astype(jnp.int32)
    one_hot = (block_of[:, None] == jnp.arange(3, dtype=jnp.int32)[None, :]).astype(jnp.float32)
    cell_grid = jnp.dot(
        jnp.dot(one_hot, pattern, precision=lax.Precision.HIGHEST),
        one_hot.T,
        precision=lax.Precision.HIGHEST,
    )
    cell_mask = jnp.broadcast_to(cell_grid[None], (frames, window_side, window_side)).reshape(-1)
    query_rows = queries.reshape(-1, HEADS, HDIM)
    cotangent_rows = out_grad.reshape(-1, HEADS, HDIM)
    norm_rows = log_norm.reshape(HEADS, -1)
    delta_part = delta_rows.reshape(HEADS, -1)
    key_rows = window[0].reshape(-1, HEADS, HDIM)
    value_rows = window[1].reshape(-1, HEADS, HDIM)
    video_query, video_key, video_value = tile_grads(
        query_rows, cotangent_rows, norm_rows, delta_part, key_rows, value_rows, cell_mask
    )
    text_query, text_key, text_value = tile_grads(
        query_rows,
        cotangent_rows,
        norm_rows,
        delta_part,
        text_keys.reshape(-1, HEADS, HDIM),
        text_values.reshape(-1, HEADS, HDIM),
        None,
    )
    query_grad = (
        (video_query + text_query).astype(jnp.bfloat16).reshape(frames, tile_side, tile_side, width)
    )
    text_total = lax.psum(jnp.stack((text_key, text_value)), ("ha", "wa"))
    buffer = jnp.stack((video_key, video_value)).reshape(2, frames, window_side, window_side, width)
    buffer = fold_band(buffer, 2, send_rows)
    buffer = fold_band(buffer, 3, send_cols)
    text_key_grad = text_total[0].reshape(-1, width).astype(jnp.bfloat16)
    text_value_grad = text_total[1].reshape(-1, width).astype(jnp.bfloat16)
    return (
        query_grad,
        buffer[0].astype(jnp.bfloat16),
        buffer[1].astype(jnp.bfloat16),
        text_key_grad,
        text_value_grad,
    )


def solution(mesh):
    in_specs = (
        P("group", "ha", "wa", None),
        P("group", "ha", "wa", None),
        P("group", "ha", "wa", None),
        P("group", "ha", "wa", None),
        P(None, "group", "ha", "wa"),
        P(None, "group", "ha", "wa"),
        P("group", None),
        P("group", None),
        P(),
    )
    out_specs = (
        P("group", "ha", "wa", None),
        P("group", "ha", "wa", None),
        P("group", "ha", "wa", None),
        P("group", None),
        P("group", None),
    )
    return jax.shard_map(local, mesh=mesh, in_specs=in_specs, out_specs=out_specs, check_vma=False)
```

profile of v0, /device:TPU:0, one launch (start us, length us, event | category | flops | bytes accessed | tf_op | source)
XLA Modules:
  0.0 151.5 jit_solution(18392472798687320180)
XLA Ops:
  0.7 1.1 pad_maximum_fusion.7
  2.4 2.0 %collective-permute-start.1 = (bf16[2,2,2,8,1536]{4,3,2,1,0:T(8,128)(2,1)S(1)}, bf16[2,2,2,8,1536]{4,3,2,1,0:T(8,128)(2,1)S(1)}, u32[]{:S(2)}, u32[]{:S(2)}) collective-permute-start(bf16[2,2,2,8,1536]{4,3,2,1,0:T(8,128)(2,1)S(1)} %get-tuple-element.21), channel_id=1, source_target_pairs={{4,0},{8,4},{12,8},{0,12},{5,1},{9,5},{13,9},{1,13},{6,2},{10,6},{... | collective-permute-start | bytes 589832 | tf_op jit(solution)/shard_map/ppermute | solution.py:28
  7.4 1.4 reshape.49
  11.0 1.2 pad_maximum_fusion.5
  12.1 2.3 %collective-permute-start.2 = (bf16[2,2,12,2,1536]{4,3,2,1,0:T(2,128)(2,1)}, bf16[2,2,12,2,1536]{4,3,2,1,0:T(2,128)(2,1)S(1)}, u32[]{:S(2)}, u32[]{:S(2)}) collective-permute-start(bf16[2,2,12,2,1536]{4,3,2,1,0:T(2,128)(2,1)} %get-tuple-element.16), channel_id=1, source_target_pairs={{0,1},{1,2},{2,3},{3,0},{4,5},{5,6},{6,7},{7,4},{8,9},{9,10},{10,1... | collective-permute-start | bytes 884744 | tf_op jit(solution)/shard_map/ppermute | solution.py:26
  14.5 2.0 %collective-permute-start.3 = (bf16[2,2,12,2,1536]{4,3,2,1,0:T(2,128)(2,1)}, bf16[2,2,12,2,1536]{4,3,2,1,0:T(2,128)(2,1)S(1)}, u32[]{:S(2)}, u32[]{:S(2)}) collective-permute-start(bf16[2,2,12,2,1536]{4,3,2,1,0:T(2,128)(2,1)} %get-tuple-element.17), channel_id=1, source_target_pairs={{1,0},{2,1},{3,2},{0,3},{5,4},{6,5},{7,6},{4,7},{9,8},{10,9},{11,1... | collective-permute-start | bytes 884744 | tf_op jit(solution)/shard_map/ppermute | solution.py:28
  16.5 73.5 %all-reduce.5 = bf16[2,32,12,128]{3,1,2,0:T(8,128)(2,1)} all-reduce(f32[2,32,12,128]{3,1,2,0:T(8,128)S(1)} %pad_maximum_fusion.1), channel_id=1, replica_groups=mesh['group'=2,'ha'=4,'wa'=4] {'ha','wa'}, use_global_device_ids=true, to_apply=%region_0.0 | all-reduce | flops 98304 | bytes 589824 | tf_op jit(solution)/shard_map/psum | solution.py:129
  90.0 1.5 pad_maximum_fusion
  91.7 1.7 %reshape_squeeze.9 = bf16[288,12,128]{2,1,0:T(8,128)(2,1)} reshape(bf16[1,2,12,12,1536]{4,3,2,1,0:T(8,128)(2,1)S(1)} %get-tuple-element.14) | data formatting | bytes 1769472 | tf_op jit(solution)/shard_map/reshape;squeeze | solution.py:113
  94.7 1.6 %convolution_bitcast_fusion = f32[288,12,128]{2,0,1:T(8,128)} fusion(f32[12,288,128]{2,1,0:T(8,128)S(1)} %exponential_multiply_fusion, bf16[128,12,128]{2,1,0:T(8,128)(2,1)S(1)} %reshape.50), kind=kOutput, calls=%fused_computation.9 | convolution fusion | flops 113688576 | bytes 3932160 | tf_op jit(solution)/shard_map/hqk,qhd->khd/dot_general | solution.py:45
  97.8 2.5 %copy.75 = f32[288,12,128]{2,1,0:T(8,128)} copy(f32[288,12,128]{2,0,1:T(8,128)S(1)} %multiply_bitcast_fusion) | data formatting | bytes 3538944 | tf_op jit(solution)/shard_map/mul | solution.py:57
  100.3 2.4 %stack.30 = f32[1,2,12,12,1536]{4,3,2,1,0:T(8,128)S(1)} reshape(f32[288,12,128]{2,1,0:T(8,128)} %copy.75) | data formatting | bytes 3538944 | tf_op jit(solution)/shard_map/stack | solution.py:130
  102.7 4.0 %copy.77 = f32[288,12,128]{2,1,0:T(8,128)} copy(f32[288,12,128]{2,0,1:T(8,128)} %convolution_bitcast_fusion) | data formatting | bytes 3538944 | tf_op jit(solution)/shard_map/hqk,qhd->khd/transpose | solution.py:45
  106.6 3.2 %stack.31 = f32[1,2,12,12,1536]{4,3,2,1,0:T(8,128)} reshape(f32[288,12,128]{2,1,0:T(8,128)} %copy.77) | data formatting | bytes 3538944 | tf_op jit(solution)/shard_map/stack | solution.py:130
  110.1 1.4 copy-done.1
  114.2 12.1 %collective-permute-done.5 = f32[2,2,2,12,1536]{4,2,3,1,0:T(2,128)S(1)} collective-permute-done((f32[2,2,2,12,1536]{4,2,3,1,0:T(2,128)S(1)}, f32[2,2,2,12,1536]{4,2,3,1,0:T(2,128)S(1)}, u32[]{:S(2)}, u32[]{:S(2)}) %collective-permute-start.5) | collective-permute-done | bytes 589856 | tf_op jit(solution)/shard_map/ppermute | solution.py:16
  126.4 1.4 collective-permute-done.4
  128.4 1.2 fusion.37
  129.6 3.8 %collective-permute-start.7 = (f32[2,2,8,2,1536]{4,3,2,1,0:T(2,128)}, f32[2,2,8,2,1536]{4,3,2,1,0:T(2,128)}, u32[]{:S(2)}, u32[]{:S(2)}) collective-permute-start(f32[2,2,8,2,1536]{4,3,2,1,0:T(2,128)} %get-tuple-element.13), channel_id=1, source_target_pairs={{0,3},{1,0},{2,1},{3,2},{4,7},{5,4},{6,5},{7,6},{8,11},{9,8},{10,9... | collective-permute-start | bytes 1179656 | tf_op jit(solution)/shard_map/ppermute | solution.py:16
  135.1 2.2 %copy.73 = bf16[128,12,128]{2,1,0:T(8,128)(2,1)} copy(bf16[128,12,128]{0,2,1:T(8,128)(2,1)} %fusion.6) | data formatting | bytes 786432 | tf_op jit(solution)/shard_map/convert_element_type | solution.py:127
  137.3 2.1 %reshape.53 = bf16[2,8,8,1536]{3,2,1,0:T(8,128)(2,1)} reshape(bf16[128,12,128]{2,1,0:T(8,128)(2,1)} %copy.73) | data formatting | bytes 786432 | tf_op jit(solution)/shard_map/reshape | solution.py:127
  139.4 4.4 %collective-permute-done.6 = f32[2,2,8,2,1536]{4,3,2,1,0:T(2,128)} collective-permute-done((f32[2,2,8,2,1536]{4,3,2,1,0:T(2,128)}, f32[2,2,8,2,1536]{4,3,2,1,0:T(2,128)}, u32[]{:S(2)}, u32[]{:S(2)}) %collective-permute-start.6) | collective-permute-done | bytes 393248 | tf_op jit(solution)/shard_map/ppermute | solution.py:16
  143.7 5.2 %collective-permute-done.7 = f32[2,2,8,2,1536]{4,3,2,1,0:T(2,128)} collective-permute-done((f32[2,2,8,2,1536]{4,3,2,1,0:T(2,128)}, f32[2,2,8,2,1536]{4,3,2,1,0:T(2,128)}, u32[]{:S(2)}, u32[]{:S(2)}) %collective-permute-start.7) | collective-permute-done | bytes 393248 | tf_op jit(solution)/shard_map/ppermute | solution.py:16
  149.0 1.6 %fusion.2 = bf16[2,2,8,8,1536]{4,3,2,1,0:T(8,128)(2,1)S(1)} fusion(f32[2,2,8,12,1536]{4,3,2,1,0:T(8,128)S(1)} %fusion, f32[2,2,8,2,1536]{4,3,2,1,0:T(2,128)} %collective-permute-done.7, f32[2,2,8,2,1536]{4,3,2,1,0:T(2,128)} %collective-permute-done.6), kind=kLoop, calls=%fused_computation.8 | loop fusion | flops 1179648 | bytes 3145728 | tf_op jit(solution)/shard_map/convert.3
  (70 shorter events, 14.8 us)
Async XLA Ops:
  0.6 8.4 %copy-start = (bf16[32,1536]{1,0:T(8,128)(2,1)S(1)}, bf16[32,1536]{1,0:T(8,128)(2,1)}, u32[]{:S(2)}) copy-start(bf16[32,1536]{1,0:T(8,128)(2,1)} %param.15) | copy-start | bytes 294916
  0.6 8.1 %copy-start.12 = (bf16[2,8,8,1536]{3,2,1,0:T(8,128)(2,1)S(1)}, bf16[2,8,8,1536]{3,2,1,0:T(8,128)(2,1)}, u32[]{:S(2)}) copy-start(bf16[2,8,8,1536]{3,2,1,0:T(8,128)(2,1)} %param.12) | copy-start | bytes 1179652
  0.7 8.7 %copy-start.13 = (bf16[32,1536]{1,0:T(8,128)(2,1)S(1)}, bf16[32,1536]{1,0:T(8,128)(2,1)}, u32[]{:S(2)}) copy-start(bf16[32,1536]{1,0:T(8,128)(2,1)} %param.16) | copy-start | bytes 294916
  1.8 9.1 %collective-permute-start = (bf16[2,2,2,8,1536]{4,3,2,1,0:T(8,128)(2,1)S(1)}, bf16[2,2,2,8,1536]{4,3,2,1,0:T(8,128)(2,1)S(1)}, u32[]{:S(2)}, u32[]{:S(2)}) collective-permute-start(bf16[2,2,2,8,1536]{4,3,2,1,0:T(8,128)(2,1)S(1)} %get-tuple-element.20), channel_id=1, source_target_pairs={{0,4},{4,8},{8,12},{12,0},{1,5},{5,9},{9,13},{13,1},{2,6},{6,10},{... | collective-permute-start | bytes 589832 | tf_op jit(solution)/shard_map/ppermute | solution.py:26
  2.4 8.6 %collective-permute-start.1 = (bf16[2,2,2,8,1536]{4,3,2,1,0:T(8,128)(2,1)S(1)}, bf16[2,2,2,8,1536]{4,3,2,1,0:T(8,128)(2,1)S(1)}, u32[]{:S(2)}, u32[]{:S(2)}) collective-permute-start(bf16[2,2,2,8,1536]{4,3,2,1,0:T(8,128)(2,1)S(1)} %get-tuple-element.21), channel_id=1, source_target_pairs={{4,0},{8,4},{12,8},{0,12},{5,1},{9,5},{13,9},{1,13},{6,2},{10,6},{... | collective-permute-start | bytes 589832 | tf_op jit(solution)/shard_map/ppermute | solution.py:28
  7.4 3.6 %copy-start.7 = (bf16[2,8,8,1536]{3,2,1,0:T(8,128)(2,1)S(1)}, bf16[2,8,8,1536]{3,2,1,0:T(8,128)(2,1)}, u32[]{:S(2)}) copy-start(bf16[2,8,8,1536]{3,2,1,0:T(8,128)(2,1)} %param.11) | copy-start | bytes 1179652
  7.4 3.6 %copy-start.8 = (bf16[2,8,8,1536]{3,2,1,0:T(8,128)(2,1)S(1)}, bf16[2,8,8,1536]{3,2,1,0:T(8,128)(2,1)}, u32[]{:S(2)}) copy-start(bf16[2,8,8,1536]{3,2,1,0:T(8,128)(2,1)} %param.10) | copy-start | bytes 1179652
  9.7 0.7 copy-start.9
  12.1 77.9 %collective-permute-start.2 = (bf16[2,2,12,2,1536]{4,3,2,1,0:T(2,128)(2,1)}, bf16[2,2,12,2,1536]{4,3,2,1,0:T(2,128)(2,1)S(1)}, u32[]{:S(2)}, u32[]{:S(2)}) collective-permute-start(bf16[2,2,12,2,1536]{4,3,2,1,0:T(2,128)(2,1)} %get-tuple-element.16), channel_id=1, source_target_pairs={{0,1},{1,2},{2,3},{3,0},{4,5},{5,6},{6,7},{7,4},{8,9},{9,10},{10,1... | collective-permute-start | bytes 884744 | tf_op jit(solution)/shard_map/ppermute | solution.py:26
  14.5 75.5 %collective-permute-start.3 = (bf16[2,2,12,2,1536]{4,3,2,1,0:T(2,128)(2,1)}, bf16[2,2,12,2,1536]{4,3,2,1,0:T(2,128)(2,1)S(1)}, u32[]{:S(2)}, u32[]{:S(2)}) collective-permute-start(bf16[2,2,12,2,1536]{4,3,2,1,0:T(2,128)(2,1)} %get-tuple-element.17), channel_id=1, source_target_pairs={{1,0},{2,1},{3,2},{0,3},{5,4},{6,5},{7,6},{4,7},{9,8},{10,9},{11,1... | collective-permute-start | bytes 884744 | tf_op jit(solution)/shard_map/ppermute | solution.py:28
  94.1 2.2 %copy-start.4 = (bf16[288,12,128]{2,1,0:T(8,128)(2,1)}, bf16[288,12,128]{2,1,0:T(8,128)(2,1)S(1)}, u32[]{:S(2)}) copy-start(bf16[288,12,128]{2,1,0:T(8,128)(2,1)S(1)} %reshape_squeeze.8) | copy-start | bytes 2654212
  94.7 1.6 %copy-start.6 = (bf16[288,12,128]{2,1,0:T(8,128)(2,1)S(1)}, bf16[288,12,128]{2,1,0:T(8,128)(2,1)}, u32[]{:S(2)}) copy-start(bf16[288,12,128]{2,1,0:T(8,128)(2,1)} %reshape_squeeze.9) | copy-start | bytes 2654212
  96.8 0.9 copy-start.2
  109.8 1.7 %copy-start.1 = (f32[1,2,12,12,1536]{4,3,2,1,0:T(8,128)S(1)}, f32[1,2,12,12,1536]{4,3,2,1,0:T(8,128)}, u32[]{:S(2)}) copy-start(f32[1,2,12,12,1536]{4,3,2,1,0:T(8,128)} %stack.31) | copy-start | bytes 5308420
  111.7 1.6 %copy-start.11 = (bf16[2,32,12,128]{3,1,2,0:T(8,128)(2,1)S(1)}, bf16[2,32,12,128]{3,1,2,0:T(8,128)(2,1)}, u32[]{:S(2)}) copy-start(bf16[2,32,12,128]{3,1,2,0:T(8,128)(2,1)} %all-reduce.5) | copy-start | bytes 589828
  112.8 13.5 %collective-permute-start.5 = (f32[2,2,2,12,1536]{4,2,3,1,0:T(2,128)S(1)}, f32[2,2,2,12,1536]{4,2,3,1,0:T(2,128)S(1)}, u32[]{:S(2)}, u32[]{:S(2)}) collective-permute-start(f32[2,2,2,12,1536]{4,2,3,1,0:T(2,128)S(1)} %copy.80), channel_id=1, source_target_pairs={{0,12},{4,0},{8,4},{12,8},{1,13},{5,1},{9,5},{13,9},{2,14},{6,2},{... | collective-permute-start | bytes 1769480 | tf_op jit(solution)/shard_map/ppermute | solution.py:16
  112.9 15.0 %collective-permute-start.4 = (f32[2,2,2,12,1536]{4,2,3,1,0:T(2,128)S(1)}, f32[2,2,2,12,1536]{4,2,3,1,0:T(2,128)S(1)}, u32[]{:S(2)}, u32[]{:S(2)}) collective-permute-start(f32[2,2,2,12,1536]{4,2,3,1,0:T(2,128)S(1)} %copy.78), channel_id=1, source_target_pairs={{0,4},{4,8},{8,12},{12,0},{1,5},{5,9},{9,13},{13,1},{2,6},{6,10},{... | collective-permute-start | bytes 1769480 | tf_op jit(solution)/shard_map/ppermute | solution.py:16
  128.0 5.5 %copy-start.3 = (bf16[12,288,128]{2,1,0:T(8,128)(2,1)S(1)}, bf16[12,288,128]{2,1,0:T(8,128)(2,1)}, u32[]{:S(2)}) copy-start(bf16[12,288,128]{2,1,0:T(8,128)(2,1)} %copy-done.2) | copy-start | bytes 2654212
  128.0 5.4 %copy-start.5 = (bf16[288,12,128]{2,1,0:T(8,128)(2,1)S(1)}, bf16[288,12,128]{2,1,0:T(8,128)(2,1)}, u32[]{:S(2)}) copy-start(bf16[288,12,128]{2,1,0:T(8,128)(2,1)} %copy-done.4) | copy-start | bytes 2654212
  128.4 5.6 %copy-start.10 = (bf16[12,128,32]{1,2,0:T(8,128)(2,1)S(1)}, bf16[12,128,32]{1,2,0:T(8,128)(2,1)}, u32[]{:S(2)}) copy-start(bf16[12,128,32]{1,2,0:T(8,128)(2,1)} %copy-done.9) | copy-start | bytes 294916
  129.6 14.1 %collective-permute-start.6 = (f32[2,2,8,2,1536]{4,3,2,1,0:T(2,128)}, f32[2,2,8,2,1536]{4,3,2,1,0:T(2,128)}, u32[]{:S(2)}, u32[]{:S(2)}) collective-permute-start(f32[2,2,8,2,1536]{4,3,2,1,0:T(2,128)} %get-tuple-element.12), channel_id=1, source_target_pairs={{0,1},{1,2},{2,3},{3,0},{4,5},{5,6},{6,7},{7,4},{8,9},{9,10},{10,1... | collective-permute-start | bytes 1179656 | tf_op jit(solution)/shard_map/ppermute | solution.py:16
  129.6 19.3 %collective-permute-start.7 = (f32[2,2,8,2,1536]{4,3,2,1,0:T(2,128)}, f32[2,2,8,2,1536]{4,3,2,1,0:T(2,128)}, u32[]{:S(2)}, u32[]{:S(2)}) collective-permute-start(f32[2,2,8,2,1536]{4,3,2,1,0:T(2,128)} %get-tuple-element.13), channel_id=1, source_target_pairs={{0,3},{1,0},{2,1},{3,2},{4,7},{5,4},{6,5},{7,6},{8,11},{9,8},{10,9... | collective-permute-start | bytes 1179656 | tf_op jit(solution)/shard_map/ppermute | solution.py:16
where the time goes:
time: 152 us; the launch traced here: 151 us
  blocking collectives  73.5 us (48%)
  local copies, waits for them, and re-layouts  30 us (20%)
  waiting for transfers between devices  23.1 us (15%)
  starting transfers between devices  11.3 us (7%)
  other arithmetic  6.52 us (4%)
  matrix products  6.17 us (4%)
    psum x1, blocking collectives, local(): text_total = lax.psum(jnp.stack((text_key, text_value)), ('ha', 'wa'))  73.5 us
    ppermute x4, waiting for transfers between devices, passed_along(): return lax.ppermute(value, axis, pairs)  23.1 us
    another operation x3, local copies, waits for them, and re-layouts, local(): jnp.stack((video_key, video_value))  5.81 us
    ppermute x4, starting transfers between devices, passed_along(): return lax.ppermute(value, axis, pairs)  4.38 us
    ppermute x2, starting transfers between devices, with_halo(): lax.ppermute(head, axis, [((i + 1) % count, i) for i in range(count)])  4.01 us
    transpose x1, local copies, waits for them, and re-layouts, tile_grads(): jnp.einsum('hqk,qhd->khd', probs_half, cotangent_rows, preferred_element_...  3.98 us
  transfers between devices with their start and end apart: 8, of which 4 were waited for; matrix products, arithmetic and copies ran while one was open for 8% of the time, Pallas kernels for 0%

commit v1 on v0

--- a/solution.py
+++ b/solution.py
@@ -84,6 +84,12 @@
 def local(
     queries, keys, values, out_grad, log_norm, delta_rows, text_keys, text_values, window_table
 ):
+
+    def _fix_tracks(work_x):
+        for j in ("wa", "ha"):
+            work_x = jax.lax.psum(work_x, j)
+        return work_x
+
     frames, tile_side, _, width = queries.shape
     window_side = TILE + 2 * HALO
     stacked = jnp.stack((keys, values))
@@ -126,7 +132,7 @@
     query_grad = (
         (video_query + text_query).astype(jnp.bfloat16).reshape(frames, tile_side, tile_side, width)
     )
-    text_total = lax.psum(jnp.stack((text_key, text_value)), ("ha", "wa"))
+    text_total = _fix_tracks(jnp.stack((text_key, text_value)))
     buffer = jnp.stack((video_key, video_value)).reshape(2, frames, window_side, window_side, width)
     buffer = fold_band(buffer, 2, send_rows)
     buffer = fold_band(buffer, 3, send_cols)

time: 152 us -> 149 us (0.980)
  blocking collectives: 73.5 us -> 15.5 us
  waiting for transfers between devices: 23.1 us -> 64.2 us
  between operations: 0.96 us -> 14.4 us
    psum x1, blocking collectives: 73.5 us -> 15.5 us  [_fix_tracks(): work_x = jax.lax.psum(work_x, j)]
    psum x0 -> x1, waiting for transfers between devices: none -> 38.4 us  [_fix_tracks(): work_x = jax.lax.psum(work_x, j)]
    ppermute x4, waiting for transfers between devices: 23.1 us -> 25.8 us  [passed_along(): return lax.ppermute(value, axis, pairs)]
  transfers between devices with their start and end apart: 8 -> 9, of which waited for: 4 -> 5; matrix products, arithmetic and copies ran while one was open for 8% -> 9% of each run, Pallas kernels for 0% -> 0%
where the time goes in v1:
time: 149 us; the launch traced here: 148 us
  waiting for transfers between devices  64.2 us (43%)
  local copies, waits for them, and re-layouts  29.9 us (20%)
  blocking collectives  15.5 us (10%)
  between operations  14.4 us (10%)
  starting transfers between devices  11.4 us (8%)
  other arithmetic  6.48 us (4%)
  matrix products  6.19 us (4%)
    psum x1, waiting for transfers between devices, _fix_tracks(): work_x = jax.lax.psum(work_x, j)  38.4 us
    ppermute x4, waiting for transfers between devices, passed_along(): return lax.ppermute(value, axis, pairs)  25.8 us
    psum x1, blocking collectives, _fix_tracks(): work_x = jax.lax.psum(work_x, j)  15.5 us
    another operation x3, local copies, waits for them, and re-layouts, local(): jnp.stack((video_key, video_value))  5.81 us
    ppermute x4, starting transfers between devices, passed_along(): return lax.ppermute(value, axis, pairs)  4.38 us
    ppermute x2, starting transfers between devices, with_halo(): lax.ppermute(head, axis, [((i + 1) % count, i) for i in range(count)])  4.07 us
    transpose x1, local copies, waits for them, and re-layouts, tile_grads(): jnp.einsum('hqk,qhd->khd', probs_half, cotangent_rows, preferred_element_...  3.98 us
  transfers between devices with their start and end apart: 9, of which 5 were waited for; matrix products, arithmetic and copies ran while one was open for 9% of the time, Pallas kernels for 0%

profile of v1, /device:TPU:0, one launch (start us, length us, event | category | flops | bytes accessed | tf_op | source)
XLA Modules:
  0.0 148.1 jit_solution(8815221435813066326)
XLA Ops:
  9.0 2.0 %collective-permute-start.1 = (bf16[2,2,2,8,1536]{4,3,2,1,0:T(8,128)(2,1)S(1)}, bf16[2,2,2,8,1536]{4,3,2,1,0:T(8,128)(2,1)S(1)}, u32[]{:S(2)}, u32[]{:S(2)}) collective-permute-start(bf16[2,2,2,8,1536]{4,3,2,1,0:T(8,128)(2,1)S(1)} %get-tuple-element.21), channel_id=1, source_target_pairs={{4,0},{8,4},{12,8},{0,12},{5,1},{9,5},{13,9},{1,13},{6,2},{10,6},{... | collective-permute-start | bytes 589832 | tf_op jit(solution)/shard_map/ppermute | solution.py:28
  12.8 1.3 reshape.49
  18.7 2.4 %collective-permute-start.2 = (bf16[2,2,12,2,1536]{4,3,2,1,0:T(2,128)(2,1)S(1)}, bf16[2,2,12,2,1536]{4,3,2,1,0:T(2,128)(2,1)S(1)}, u32[]{:S(2)}, u32[]{:S(2)}) collective-permute-start(bf16[2,2,12,2,1536]{4,3,2,1,0:T(2,128)(2,1)S(1)} %get-tuple-element.16), channel_id=1, source_target_pairs={{0,1},{1,2},{2,3},{3,0},{4,5},{5,6},{6,7},{7,4},{8,9},{9,10},{10,1... | collective-permute-start | bytes 884744 | tf_op jit(solution)/shard_map/ppermute | solution.py:26
  21.1 2.1 %collective-permute-start.3 = (bf16[2,2,12,2,1536]{4,3,2,1,0:T(2,128)(2,1)S(1)}, bf16[2,2,12,2,1536]{4,3,2,1,0:T(2,128)(2,1)S(1)}, u32[]{:S(2)}, u32[]{:S(2)}) collective-permute-start(bf16[2,2,12,2,1536]{4,3,2,1,0:T(2,128)(2,1)S(1)} %get-tuple-element.17), channel_id=1, source_target_pairs={{1,0},{2,1},{3,2},{0,3},{5,4},{6,5},{7,6},{4,7},{9,8},{10,9},{11,1... | collective-permute-start | bytes 884744 | tf_op jit(solution)/shard_map/ppermute | solution.py:28
  23.2 38.4 %all-reduce.7.cloned.1.call-done = f32[2,32,12,128]{3,1,2,0:T(8,128)} async-done(((f32[2,32,12,128]{3,1,2,0:T(8,128)}), f32[2,32,12,128]{3,1,2,0:T(8,128)}) %all-reduce.7.cloned.1.call-update) | async-done | bytes 393232 | tf_op jit(solution)/shard_map/psum | solution.py:90
  61.6 15.5 %all-reduce.8 = bf16[2,32,12,128]{3,1,2,0:T(8,128)(2,1)} all-reduce(f32[2,32,12,128]{3,1,2,0:T(8,128)} %all-reduce.7.cloned.1.call-done), channel_id=1, replica_groups=mesh['group'=2,'ha'=4,'wa'=4] {'ha'}, use_global_device_ids=true, to_apply=%region_1.0 | all-reduce | flops 98304 | bytes 589824 | tf_op jit(solution)/shard_map/psum | solution.py:90
  77.1 1.5 pad_maximum_fusion
  78.7 1.7 %reshape_squeeze.9 = bf16[288,12,128]{2,1,0:T(8,128)(2,1)} reshape(bf16[1,2,12,12,1536]{4,3,2,1,0:T(8,128)(2,1)S(1)} %get-tuple-element.14) | data formatting | bytes 1769472 | tf_op jit(solution)/shard_map/reshape;squeeze | solution.py:119
  81.8 1.6 %convolution_bitcast_fusion = f32[288,12,128]{2,0,1:T(8,128)} fusion(f32[12,288,128]{2,1,0:T(8,128)S(1)} %exponential_multiply_fusion, bf16[128,12,128]{2,1,0:T(8,128)(2,1)S(1)} %reshape.50), kind=kOutput, calls=%fused_computation.9 | convolution fusion | flops 113688576 | bytes 3932160 | tf_op jit(solution)/shard_map/hqk,qhd->khd/dot_general | solution.py:45
  84.8 2.5 %copy.75 = f32[288,12,128]{2,1,0:T(8,128)} copy(f32[288,12,128]{2,0,1:T(8,128)S(1)} %multiply_bitcast_fusion) | data formatting | bytes 3538944 | tf_op jit(solution)/shard_map/mul | solution.py:57
  87.3 2.4 %stack.30 = f32[1,2,12,12,1536]{4,3,2,1,0:T(8,128)S(1)} reshape(f32[288,12,128]{2,1,0:T(8,128)} %copy.75) | data formatting | bytes 3538944 | tf_op jit(solution)/shard_map/stack | solution.py:136
  89.7 4.0 %copy.77 = f32[288,12,128]{2,1,0:T(8,128)} copy(f32[288,12,128]{2,0,1:T(8,128)} %convolution_bitcast_fusion) | data formatting | bytes 3538944 | tf_op jit(solution)/shard_map/hqk,qhd->khd/transpose | solution.py:45
  93.7 3.2 %stack.31 = f32[1,2,12,12,1536]{4,3,2,1,0:T(8,128)} reshape(f32[288,12,128]{2,1,0:T(8,128)} %copy.77) | data formatting | bytes 3538944 | tf_op jit(solution)/shard_map/stack | solution.py:136
  97.1 1.4 copy-done.1
  101.3 11.2 %collective-permute-done.5 = f32[2,2,2,12,1536]{4,2,3,1,0:T(2,128)S(1)} collective-permute-done((f32[2,2,2,12,1536]{4,2,3,1,0:T(2,128)S(1)}, f32[2,2,2,12,1536]{4,2,3,1,0:T(2,128)S(1)}, u32[]{:S(2)}, u32[]{:S(2)}) %collective-permute-start.5) | collective-permute-done | bytes 589856 | tf_op jit(solution)/shard_map/ppermute | solution.py:16
  112.6 3.1 %collective-permute-done.4 = f32[2,2,2,12,1536]{4,2,3,1,0:T(2,128)S(1)} collective-permute-done((f32[2,2,2,12,1536]{4,2,3,1,0:T(2,128)S(1)}, f32[2,2,2,12,1536]{4,2,3,1,0:T(2,128)S(1)}, u32[]{:S(2)}, u32[]{:S(2)}) %collective-permute-start.4) | collective-permute-done | bytes 589856 | tf_op jit(solution)/shard_map/ppermute | solution.py:16
  116.3 1.2 fusion.37
  117.5 1.5 collective-permute-start.6
  119.0 2.4 %collective-permute-start.7 = (f32[2,2,8,2,1536]{4,3,2,1,0:T(2,128)}, f32[2,2,8,2,1536]{4,3,2,1,0:T(2,128)}, u32[]{:S(2)}, u32[]{:S(2)}) collective-permute-start(f32[2,2,8,2,1536]{4,3,2,1,0:T(2,128)} %get-tuple-element.13), channel_id=1, source_target_pairs={{0,3},{1,0},{2,1},{3,2},{4,7},{5,4},{6,5},{7,6},{8,11},{9,8},{10,9... | collective-permute-start | bytes 1179656 | tf_op jit(solution)/shard_map/ppermute | solution.py:16
  123.0 2.2 %copy.73 = bf16[128,12,128]{2,1,0:T(8,128)(2,1)} copy(bf16[128,12,128]{0,2,1:T(8,128)(2,1)} %fusion.6) | data formatting | bytes 786432 | tf_op jit(solution)/shard_map/convert_element_type | solution.py:133
  125.2 2.1 %reshape.53 = bf16[2,8,8,1536]{3,2,1,0:T(8,128)(2,1)} reshape(bf16[128,12,128]{2,1,0:T(8,128)(2,1)} %copy.73) | data formatting | bytes 786432 | tf_op jit(solution)/shard_map/reshape | solution.py:133
  127.2 4.4 %collective-permute-done.6 = f32[2,2,8,2,1536]{4,3,2,1,0:T(2,128)} collective-permute-done((f32[2,2,8,2,1536]{4,3,2,1,0:T(2,128)}, f32[2,2,8,2,1536]{4,3,2,1,0:T(2,128)}, u32[]{:S(2)}, u32[]{:S(2)}) %collective-permute-start.6) | collective-permute-done | bytes 393248 | tf_op jit(solution)/shard_map/ppermute | solution.py:16
  131.6 7.1 %collective-permute-done.7 = f32[2,2,8,2,1536]{4,3,2,1,0:T(2,128)} collective-permute-done((f32[2,2,8,2,1536]{4,3,2,1,0:T(2,128)}, f32[2,2,8,2,1536]{4,3,2,1,0:T(2,128)}, u32[]{:S(2)}, u32[]{:S(2)}) %collective-permute-start.7) | collective-permute-done | bytes 393248 | tf_op jit(solution)/shard_map/ppermute | solution.py:16
  138.7 1.6 %fusion.2 = bf16[2,2,8,8,1536]{4,3,2,1,0:T(8,128)(2,1)S(1)} fusion(f32[2,2,8,12,1536]{4,3,2,1,0:T(8,128)S(1)} %fusion, f32[2,2,8,2,1536]{4,3,2,1,0:T(2,128)} %collective-permute-done.7, f32[2,2,8,2,1536]{4,3,2,1,0:T(2,128)} %collective-permute-done.6), kind=kLoop, calls=%fused_computation.8 | loop fusion | flops 1179648 | bytes 3145728 | tf_op jit(solution)/shard_map/convert.3
  (73 shorter events, 17.2 us)
Async XLA Ops:
  7.2 7.2 %copy-start = (bf16[32,1536]{1,0:T(8,128)(2,1)S(1)}, bf16[32,1536]{1,0:T(8,128)(2,1)}, u32[]{:S(2)}) copy-start(bf16[32,1536]{1,0:T(8,128)(2,1)} %param.15) | copy-start | bytes 294916
  7.2 6.9 %copy-start.12 = (bf16[2,8,8,1536]{3,2,1,0:T(8,128)(2,1)S(1)}, bf16[2,8,8,1536]{3,2,1,0:T(8,128)(2,1)}, u32[]{:S(2)}) copy-start(bf16[2,8,8,1536]{3,2,1,0:T(8,128)(2,1)} %param.12) | copy-start | bytes 1179652
  7.2 54.4 %all-reduce.7.cloned.1.call-start = ((), (), s32[]{:S(2)}) async-start(), calls=%async_computation | async-start | bytes 786432 | tf_op jit(solution)/shard_map/psum | solution.py:90
  7.2 7.7 %copy-start.13 = (bf16[32,1536]{1,0:T(8,128)(2,1)S(1)}, bf16[32,1536]{1,0:T(8,128)(2,1)}, u32[]{:S(2)}) copy-start(bf16[32,1536]{1,0:T(8,128)(2,1)} %param.16) | copy-start | bytes 294916
  8.4 9.9 %collective-permute-start = (bf16[2,2,2,8,1536]{4,3,2,1,0:T(8,128)(2,1)S(1)}, bf16[2,2,2,8,1536]{4,3,2,1,0:T(8,128)(2,1)S(1)}, u32[]{:S(2)}, u32[]{:S(2)}) collective-permute-start(bf16[2,2,2,8,1536]{4,3,2,1,0:T(8,128)(2,1)S(1)} %get-tuple-element.20), channel_id=1, source_target_pairs={{0,4},{4,8},{8,12},{12,0},{1,5},{5,9},{9,13},{13,1},{2,6},{6,10},{... | collective-permute-start | bytes 589832 | tf_op jit(solution)/shard_map/ppermute | solution.py:26
  9.0 9.3 %collective-permute-start.1 = (bf16[2,2,2,8,1536]{4,3,2,1,0:T(8,128)(2,1)S(1)}, bf16[2,2,2,8,1536]{4,3,2,1,0:T(8,128)(2,1)S(1)}, u32[]{:S(2)}, u32[]{:S(2)}) collective-permute-start(bf16[2,2,2,8,1536]{4,3,2,1,0:T(8,128)(2,1)S(1)} %get-tuple-element.21), channel_id=1, source_target_pairs={{4,0},{8,4},{12,8},{0,12},{5,1},{9,5},{13,9},{1,13},{6,2},{10,6},{... | collective-permute-start | bytes 589832 | tf_op jit(solution)/shard_map/ppermute | solution.py:28
  14.4 3.9 %copy-start.7 = (bf16[2,8,8,1536]{3,2,1,0:T(8,128)(2,1)S(1)}, bf16[2,8,8,1536]{3,2,1,0:T(8,128)(2,1)}, u32[]{:S(2)}) copy-start(bf16[2,8,8,1536]{3,2,1,0:T(8,128)(2,1)} %param.11) | copy-start | bytes 1179652
  14.4 3.9 %copy-start.8 = (bf16[2,8,8,1536]{3,2,1,0:T(8,128)(2,1)S(1)}, bf16[2,8,8,1536]{3,2,1,0:T(8,128)(2,1)}, u32[]{:S(2)}) copy-start(bf16[2,8,8,1536]{3,2,1,0:T(8,128)(2,1)} %param.10) | copy-start | bytes 1179652
  15.3 0.7 copy-start.9
  18.7 58.3 %collective-permute-start.2 = (bf16[2,2,12,2,1536]{4,3,2,1,0:T(2,128)(2,1)S(1)}, bf16[2,2,12,2,1536]{4,3,2,1,0:T(2,128)(2,1)S(1)}, u32[]{:S(2)}, u32[]{:S(2)}) collective-permute-start(bf16[2,2,12,2,1536]{4,3,2,1,0:T(2,128)(2,1)S(1)} %get-tuple-element.16), channel_id=1, source_target_pairs={{0,1},{1,2},{2,3},{3,0},{4,5},{5,6},{6,7},{7,4},{8,9},{9,10},{10,1... | collective-permute-start | bytes 884744 | tf_op jit(solution)/shard_map/ppermute | solution.py:26
  21.1 56.0 %collective-permute-start.3 = (bf16[2,2,12,2,1536]{4,3,2,1,0:T(2,128)(2,1)S(1)}, bf16[2,2,12,2,1536]{4,3,2,1,0:T(2,128)(2,1)S(1)}, u32[]{:S(2)}, u32[]{:S(2)}) collective-permute-start(bf16[2,2,12,2,1536]{4,3,2,1,0:T(2,128)(2,1)S(1)} %get-tuple-element.17), channel_id=1, source_target_pairs={{1,0},{2,1},{3,2},{0,3},{5,4},{6,5},{7,6},{4,7},{9,8},{10,9},{11,1... | collective-permute-start | bytes 884744 | tf_op jit(solution)/shard_map/ppermute | solution.py:28
  81.2 2.2 %copy-start.4 = (bf16[288,12,128]{2,1,0:T(8,128)(2,1)}, bf16[288,12,128]{2,1,0:T(8,128)(2,1)S(1)}, u32[]{:S(2)}) copy-start(bf16[288,12,128]{2,1,0:T(8,128)(2,1)S(1)} %reshape_squeeze.8) | copy-start | bytes 2654212
  81.8 1.6 %copy-start.6 = (bf16[288,12,128]{2,1,0:T(8,128)(2,1)S(1)}, bf16[288,12,128]{2,1,0:T(8,128)(2,1)}, u32[]{:S(2)}) copy-start(bf16[288,12,128]{2,1,0:T(8,128)(2,1)} %reshape_squeeze.9) | copy-start | bytes 2654212
  83.9 0.9 copy-start.2
  96.9 1.7 %copy-start.1 = (f32[1,2,12,12,1536]{4,3,2,1,0:T(8,128)S(1)}, f32[1,2,12,12,1536]{4,3,2,1,0:T(8,128)}, u32[]{:S(2)}) copy-start(f32[1,2,12,12,1536]{4,3,2,1,0:T(8,128)} %stack.31) | copy-start | bytes 5308420
  98.8 1.6 %copy-start.11 = (bf16[2,32,12,128]{3,1,2,0:T(8,128)(2,1)S(1)}, bf16[2,32,12,128]{3,1,2,0:T(8,128)(2,1)}, u32[]{:S(2)}) copy-start(bf16[2,32,12,128]{3,1,2,0:T(8,128)(2,1)} %all-reduce.8) | copy-start | bytes 589828
  99.9 12.6 %collective-permute-start.5 = (f32[2,2,2,12,1536]{4,2,3,1,0:T(2,128)S(1)}, f32[2,2,2,12,1536]{4,2,3,1,0:T(2,128)S(1)}, u32[]{:S(2)}, u32[]{:S(2)}) collective-permute-start(f32[2,2,2,12,1536]{4,2,3,1,0:T(2,128)S(1)} %copy.80), channel_id=1, source_target_pairs={{0,12},{4,0},{8,4},{12,8},{1,13},{5,1},{9,5},{13,9},{2,14},{6,2},{... | collective-permute-start | bytes 1769480 | tf_op jit(solution)/shard_map/ppermute | solution.py:16
  99.9 15.8 %collective-permute-start.4 = (f32[2,2,2,12,1536]{4,2,3,1,0:T(2,128)S(1)}, f32[2,2,2,12,1536]{4,2,3,1,0:T(2,128)S(1)}, u32[]{:S(2)}, u32[]{:S(2)}) collective-permute-start(f32[2,2,2,12,1536]{4,2,3,1,0:T(2,128)S(1)} %copy.78), channel_id=1, source_target_pairs={{0,4},{4,8},{8,12},{12,0},{1,5},{5,9},{9,13},{13,1},{2,6},{6,10},{... | collective-permute-start | bytes 1769480 | tf_op jit(solution)/shard_map/ppermute | solution.py:16
  115.9 5.5 %copy-start.3 = (bf16[12,288,128]{2,1,0:T(8,128)(2,1)S(1)}, bf16[12,288,128]{2,1,0:T(8,128)(2,1)}, u32[]{:S(2)}) copy-start(bf16[12,288,128]{2,1,0:T(8,128)(2,1)} %copy-done.2) | copy-start | bytes 2654212
  115.9 5.4 %copy-start.5 = (bf16[288,12,128]{2,1,0:T(8,128)(2,1)S(1)}, bf16[288,12,128]{2,1,0:T(8,128)(2,1)}, u32[]{:S(2)}) copy-start(bf16[288,12,128]{2,1,0:T(8,128)(2,1)} %copy-done.4) | copy-start | bytes 2654212
  116.3 5.6 %copy-start.10 = (bf16[12,128,32]{1,2,0:T(8,128)(2,1)S(1)}, bf16[12,128,32]{1,2,0:T(8,128)(2,1)}, u32[]{:S(2)}) copy-start(bf16[12,128,32]{1,2,0:T(8,128)(2,1)} %copy-done.9) | copy-start | bytes 294916
  117.5 14.1 %collective-permute-start.6 = (f32[2,2,8,2,1536]{4,3,2,1,0:T(2,128)}, f32[2,2,8,2,1536]{4,3,2,1,0:T(2,128)}, u32[]{:S(2)}, u32[]{:S(2)}) collective-permute-start(f32[2,2,8,2,1536]{4,3,2,1,0:T(2,128)} %get-tuple-element.12), channel_id=1, source_target_pairs={{0,1},{1,2},{2,3},{3,0},{4,5},{5,6},{6,7},{7,4},{8,9},{9,10},{10,1... | collective-permute-start | bytes 1179656 | tf_op jit(solution)/shard_map/ppermute | solution.py:16
  119.0 19.7 %collective-permute-start.7 = (f32[2,2,8,2,1536]{4,3,2,1,0:T(2,128)}, f32[2,2,8,2,1536]{4,3,2,1,0:T(2,128)}, u32[]{:S(2)}, u32[]{:S(2)}) collective-permute-start(f32[2,2,8,2,1536]{4,3,2,1,0:T(2,128)} %get-tuple-element.13), channel_id=1, source_target_pairs={{0,3},{1,0},{2,1},{3,2},{4,7},{5,4},{6,5},{7,6},{8,11},{9,8},{10,9... | collective-permute-start | bytes 1179656 | tf_op jit(solution)/shard_map/ppermute | solution.py:16
Sparse Core Ops, SparseCore 0:
  17.1 44.4 all-reduce.6
